TPU v7x, 32 devices: a 4x4x1 block of a 4x4x8 slice. The times are simulated.
32 devices in a mesh: dp: 1 (over z), tp: 32 (over y, x, core).
Axes of the slice: x: 4, y: 4, z: 1, core: 2. Of those that a mesh axis runs over, the one named last changes fastest.
The devices are a block of a 4x4x8 slice.
Arguments:
- hidden: bfloat16 [16384, 1536], P(('dp', 'tp'))
- ln_gain: float32 [1536], replicated
- ln_bias: float32 [1536], replicated
- embed: bfloat16 [16384, 1536], P('tp')
- targets: int32 [16384], P(('dp', 'tp'))
- loss_mask: int32 [16384], P(('dp', 'tp'))
Outputs:
- output 1: float32 [16384], P(('dp', 'tp'))
- output 2: float32 [1], P('dp')
- output 3: bfloat16 [16384, 1536], P(('dp', 'tp'))
- output 4: float32 [16384, 1536], P(('dp', 'tp'))
- output 5: float32 [1536], P('dp')
- output 6: float32 [1536], P('dp')
All inputs are finite; a program needn't handle non-finite values.
Results may differ from a plain program's by a relative error of at most 0.001.
Values are sent between devices in bfloat16 or wider.
A program may use at most 768 MiB of HBM per device.

v0:
```python
import jax
import jax.numpy as jnp
from jax import lax
from jax.sharding import PartitionSpec as P

LN_EPS = 1e-5


def layer_norm(hidden, ln_gain, ln_bias):
    h_f32 = hidden.astype(jnp.float32)
    centred = h_f32 - jnp.mean(h_f32, axis=-1, keepdims=True)
    inv_std = lax.rsqrt(jnp.mean(centred * centred, axis=-1, keepdims=True) + LN_EPS)
    x_hat = centred * inv_std
    return x_hat, inv_std, (x_hat * ln_gain + ln_bias).astype(jnp.bfloat16)


def norm_backward(d_normed, x_hat, inv_std, ln_gain):
    value_a6 = d_normed * ln_gain
    centre_term = jnp.mean(value_a6, axis=-1, keepdims=True)
    proj_term = jnp.mean(value_a6 * x_hat, axis=-1, keepdims=True)
    return (inv_std * (value_a6 - centre_term - x_hat * proj_term)).astype(jnp.bfloat16)


def solution(mesh):
    group = mesh.shape['tp']

    def body(hidden, ln_gain, ln_bias, embed, targets, loss_mask):
        tokens = hidden.shape[0]
        shard_vocab = embed.shape[0]
        rank = lax.axis_index('tp')
        x_hat, inv_std, normed = layer_norm(hidden, ln_gain, ln_bias)
        gathered = lax.all_gather(normed, 'tp', tiled=True)
        all_targets = lax.all_gather(targets, 'tp', tiled=True)
        all_weights = lax.all_gather(loss_mask, 'tp', tiled=True).astype(jnp.float32)
        count = lax.psum(jnp.sum(loss_mask.astype(jnp.float32)), 'tp')
        logits = jnp.einsum('sd,vd->sv', gathered, embed, preferred_element_type=jnp.float32)
        vocab_ids = rank * shard_vocab + lax.broadcasted_iota(jnp.int32, (1, shard_vocab), 1)
        onehot = vocab_ids == all_targets[:, None]
        local_max = jnp.max(logits, axis=-1)
        local_sum = jnp.sum(jnp.exp(logits - local_max[:, None]), axis=-1)
        local_target = jnp.sum(jnp.where(onehot, logits, 0.0), axis=-1)
        global_max = lax.pmax(local_max, 'tp')
        combined = lax.psum(jnp.stack([local_sum * jnp.exp(local_max - global_max), local_target]), 'tp')
        log_norm = global_max + jnp.log(combined[0])
        all_loss = (log_norm - combined[1]) * all_weights
        mean_loss = jnp.sum(all_loss) / count
        d_logits = ((jnp.exp(logits - log_norm[:, None]) - onehot.astype(jnp.float32)) * (all_weights / count)[:, None]).astype(jnp.bfloat16)
        d_embed = jnp.einsum('sv,sd->vd', d_logits, gathered, preferred_element_type=jnp.float32)
        d_part = jnp.einsum('sv,vd->sd', d_logits, embed, preferred_element_type=jnp.float32)
        d_normed = lax.psum_scatter(d_part, 'tp', scatter_dimension=0, tiled=True)
        norm_grads = lax.psum(jnp.stack([jnp.sum(d_normed * x_hat, axis=0), jnp.sum(d_normed, axis=0)]), 'tp')
        d_hidden = norm_backward(d_normed, x_hat, inv_std, ln_gain)
        own_loss = all_loss.reshape(group, tokens)[rank]
        return own_loss, mean_loss.reshape(1), d_hidden, d_embed, norm_grads[0], norm_grads[1]

    token_rows = P(('dp', 'tp'))
    token_mat = P(('dp', 'tp'), None)
    return jax.shard_map(body, mesh=mesh, in_specs=(token_mat, P(), P(), P('tp', None), token_rows, token_rows), out_specs=(token_rows, P('dp'), token_mat, token_mat, P('dp'), P('dp')), check_vma=False)
```

profile of v0, /device:TPU:97, one launch (start us, length us, event | category | flops | bytes accessed | tf_op | source)
XLA Modules:
  0.0 894.7 jit_solution(17689131280749220356)
XLA Ops:
  7.2 0.1 all-gather.4.cloned.1.call-start
  7.3 1.8 convert_reduce_fusion
  9.2 2.0 fusion.17
  11.2 1.8 fusion.11
  13.0 0.1 all-gather.4.cloned.1.call-update
  13.0 0.1 all-reduce.3.cloned.1.call-start
  13.1 32.9 %all-gather = s32[32,1,512]{2,1,0:T(1,128)S(1)} all-gather(s32[1,1,512]{2,1,0:T(1,128)S(1)} %bitcast.24), channel_id=1, replica_groups=mesh['dp'=1,'tp'=32] {'tp'}, dimensions={0}, use_global_device_ids=true | all-gather | bytes 67584 | tf_op jit(solution)/shard_map/all_gather | solution.py:33
  46.1 123.9 %all-gather.4.cloned.1.call-done = bf16[16384,1536]{1,0:T(8,128)(2,1)} async-done(((bf16[512,1536]{1,0:T(8,128)(2,1)}), bf16[16384,1536]{1,0:T(8,128)(2,1)}) %all-gather.4.cloned.1.call-update) | async-done | bytes 50331664 | tf_op jit(solution)/shard_map/all_gather | solution.py:32
  170.0 36.3 %fusion.23 = (f32[16384]{0:T(1024)}, f32[16384,512]{0,1:T(8,128)}) fusion(bf16[16384,1536]{1,0:T(8,128)(2,1)} %all-gather.4.cloned.1.call-done, bf16[512,1536]{1,0:T(8,128)(2,1)S(1)} %copy-done), kind=kOutput, calls=%fused_computation.42 | convolution fusion | flops 25778176000 | bytes 85524480 | tf_op jit(solution)/shard_map/sd,vd->sv/dot_general | solution.py:36
  206.3 0.1 all-reduce.3.cloned.1.call-update
  206.4 0.1 all-reduce.5.cloned.1.call-start
  206.5 16.2 %exponential_reduce_fusion = (f32[16384]{0:T(1024)S(1)}, f32[16384]{0:T(1024)S(1)}) fusion(f32[16384,512]{0,1:T(8,128)} %get-tuple-element.21, f32[16384]{0:T(1024)} %get-tuple-element.20, s32[16384]{0:T(1024)S(1)} %bitcast.15, s32[512]{0:T(512)S(1)} %iota_add_fusion), kind=kLoop, calls=%fused_computation.6 | loop fusion | flops 41910272 | bytes 33818624 | tf_op jit(solution)/shard_map/reduce_sum | solution.py:40
  222.6 73.6 %all-reduce.3.cloned.1.call-done = f32[16384]{0:T(1024)} async-done(((f32[16384]{0:T(1024)}), f32[16384]{0:T(1024)}) %all-reduce.3.cloned.1.call-update) | async-done | bytes 65552 | tf_op jit(solution)/shard_map/pmax | solution.py:42
  296.3 0.9 exponential_multiply_fusion
  297.1 0.8 pad_maximum_fusion
  297.9 0.1 all-reduce.5.cloned.1.call-update
  298.0 0.1 reduce-scatter.2.cloned.1.call-start
  298.0 0.6 convert_reduce_fusion.1
  298.6 46.8 %psum.22 = f32[]{:T(128)} all-reduce(f32[]{:T(128)} %convert_reduce_fusion.1), channel_id=1, replica_groups=mesh['dp'=1,'tp'=32] {'tp'}, use_global_device_ids=true, to_apply=%region_9.10 | all-reduce | flops 1 | bytes 8 | tf_op jit(solution)/shard_map/psum | solution.py:35
  345.4 26.8 %all-gather.1 = s32[32,1,512]{2,1,0:T(1,128)S(1)} all-gather(s32[1,1,512]{2,1,0:T(1,128)S(1)} %bitcast.23), channel_id=1, replica_groups=mesh['dp'=1,'tp'=32] {'tp'}, dimensions={0}, use_global_device_ids=true | all-gather | bytes 67584 | tf_op jit(solution)/shard_map/all_gather | solution.py:34
  372.2 20.3 %all-reduce.5.cloned.1.call-done = f32[2,16384]{1,0:T(2,128)} async-done(((f32[2,16384]{1,0:T(2,128)}), f32[2,16384]{1,0:T(2,128)}) %all-reduce.5.cloned.1.call-update) | async-done | bytes 131088 | tf_op jit(solution)/shard_map/psum | solution.py:43
  392.5 1.1 slice_log_fusion
  393.7 2.1 fusion.22
  395.8 48.6 %fusion.20 = f32[16384,1536]{1,0:T(8,128)} fusion(bf16[512,1536]{1,0:T(8,128)(2,1)S(1)} %copy-done, f32[16384,512]{0,1:T(8,128)} %get-tuple-element.21, f32[16384]{0:T(1024)S(1)} %get-tuple-element.19, f32[16384]{0:T(1024)S(1)} %get-tuple-element.16, s32[16384]{0:T(1024)S(1)} %bitcast.16, s32[512]{0:T(512)S(1)} %iota_add_fusion), kind=kOutput, calls=%fused_computation.40 | convolution fusion | flops 25820135424 | bytes 135989248 | tf_op jit(solution)/shard_map/sv,vd->sd/dot_general | solution.py:49
  444.4 0.1 reduce-scatter.2.cloned.1.call-update
  445.8 0.6 constant_dynamic-slice_fusion
  446.4 36.0 %fusion.18 = f32[512,1536]{1,0:T(8,128)} fusion(bf16[16384,1536]{1,0:T(8,128)(2,1)} %all-gather.4.cloned.1.call-done, f32[16384,512]{0,1:T(8,128)} %get-tuple-element.21, f32[16384]{0:T(1024)S(1)} %get-tuple-element.19, f32[16384]{0:T(1024)S(1)} %get-tuple-element.16, s32[16384]{0:T(1024)S(1)} %bitcast.17, s32[512]{0:T(512)S(1)} %iota_add_fusion), kind=kOutput, calls=%fused_computation.39 | convolution fusion | flops 25820135424 | bytes 87230464 | tf_op jit(solution)/shard_map/sv,sd->vd/dot_general | solution.py:48
  482.4 351.2 %reduce-scatter.2.cloned.1.call-done = f32[512,1536]{1,0:T(8,128)} async-done(((f32[16384,1536]{1,0:T(8,128)}), f32[512,1536]{1,0:T(8,128)}) %reduce-scatter.2.cloned.1.call-update) | async-done | bytes 3145744 | tf_op jit(solution)/shard_map/reduce_scatter | solution.py:50
  833.6 3.3 fusion.16
  836.9 45.4 %psum.23 = f32[2,1536]{1,0:T(2,128)S(1)} all-reduce(f32[2,1536]{1,0:T(2,128)S(1)} %pad_maximum_fusion.1), channel_id=1, replica_groups=mesh['dp'=1,'tp'=32] {'tp'}, use_global_device_ids=true, to_apply=%region_15.16 | all-reduce | flops 3072 | bytes 24576 | tf_op jit(solution)/shard_map/psum | solution.py:51
  882.3 0.6 slice_reduce_fusion
  883.0 4.1 fusion.15
  (37 shorter events, 0.2 us)
Async XLA Ops:
  7.2 162.8 %copy-start = (bf16[512,1536]{1,0:T(8,128)(2,1)S(1)}, bf16[512,1536]{1,0:T(8,128)(2,1)}, u32[]{:S(2)}) copy-start(bf16[512,1536]{1,0:T(8,128)(2,1)} %param.9) | copy-start | bytes 4718596
  7.2 3.9 copy-start.2
  7.2 3.9 copy-start.5
  7.2 3.9 copy-start.11
  7.2 162.8 %all-gather.4.cloned.1.call-start = ((), (), s32[]{:S(2)}) async-start(), calls=%async_computation.1 | async-start | bytes 51904512 | tf_op jit(solution)/shard_map/all_gather | solution.py:32
  9.1 3.9 copy-start.7
  9.2 4.0 copy-start.13
  11.2 1.9 copy-start.9
  13.0 283.2 %all-reduce.3.cloned.1.call-start = ((), (), s32[]{:S(2)}) async-start(), calls=%async_computation.2 | async-start | bytes 131072 | tf_op jit(solution)/shard_map/pmax | solution.py:42
  206.4 186.2 %all-reduce.5.cloned.1.call-start = ((), (), s32[]{:S(2)}) async-start(), calls=%async_computation.3 | async-start | bytes 262144 | tf_op jit(solution)/shard_map/psum | solution.py:43
  206.4 89.8 %copy-start.4 = (f32[16384]{0:T(1024)S(1)}, f32[16384]{0:T(1024)}, u32[]{:S(2)}) copy-start(f32[16384]{0:T(1024)} %get-tuple-element.20) | copy-start | bytes 196612
  206.4 91.6 %copy-start.12 = (s32[512]{0:T(512)S(1)}, s32[512]{0:T(512)}, u32[]{:S(2)}) copy-start(s32[512]{0:T(512)} %param.11) | copy-start | bytes 6148
  298.0 535.6 %reduce-scatter.2.cloned.1.call-start = ((), (), s32[]{:S(2)}) async-start(), calls=%async_computation.4 | async-start | bytes 103809024 | tf_op jit(solution)/shard_map/reduce_scatter | solution.py:50
  446.4 387.2 %copy-start.3 = (bf16[512,1536]{1,0:T(8,128)(2,1)S(1)}, bf16[512,1536]{1,0:T(8,128)(2,1)}, u32[]{:S(2)}) copy-start(bf16[512,1536]{1,0:T(8,128)(2,1)} %param.6) | copy-start | bytes 4718596
  446.4 387.2 %copy-start.6 = (f32[1536]{0:T(1024)S(1)}, f32[1536]{0:T(1024)}, u32[]{:S(2)}) copy-start(f32[1536]{0:T(1024)} %param.7) | copy-start | bytes 18436
  446.4 387.2 %copy-start.8 = (f32[512]{0:T(512)S(1)}, f32[512]{0:T(512)}, u32[]{:S(2)}) copy-start(f32[512]{0:T(512)} %copy-done.7) | copy-start | bytes 6148
  446.4 387.2 %copy-start.10 = (f32[512]{0:T(512)S(1)}, f32[512]{0:T(512)}, u32[]{:S(2)}) copy-start(f32[512]{0:T(512)} %copy-done.9) | copy-start | bytes 6148
  883.0 4.1 copy-start.1
Sparse Core Ops, SparseCore 0:
  13.1 156.7 all-gather.3
  206.5 89.7 all-reduce.2
  300.1 92.3 all-reduce.4
  444.6 388.9 reduce-scatter.1
where the time goes:
time: 895 us
  waiting for transfers between devices  569 us (64%)
  blocking collectives  152 us (17%)
  matrix products  121 us (14%)
  other arithmetic  33.5 us (4%)
  between operations  16.5 us (2%)
    reduce_scatter x1, waiting for transfers between devices, body(): d_normed = lax.psum_scatter(d_part, 'tp', scatter_dimension=0, tiled=True)  351 us
    all_gather x1, waiting for transfers between devices, body(): gathered = lax.all_gather(normed, 'tp', tiled=True)  124 us
    pmax x1, waiting for transfers between devices, body(): global_max = lax.pmax(local_max, 'tp')  73.6 us
    dot_general x1, matrix products, body(): jnp.einsum('sv,vd->sd', d_logits, embed, preferred_element_type=jnp.float32)  48.6 us
    psum x1, blocking collectives, body(): count = lax.psum(jnp.sum(loss_mask.astype(jnp.float32)), 'tp')  46.8 us
    psum x1, blocking collectives, body(): lax.psum(jnp.stack([jnp.sum(d_normed * x_hat, axis=0), jnp.sum(d_normed,...  45.4 us
    dot_general x1, matrix products, body(): jnp.einsum('sd,vd->sv', gathered, embed, preferred_element_type=jnp.float32)  36.3 us
    dot_general x1, matrix products, body(): jnp.einsum('sv,sd->vd', d_logits, gathered, preferred_element_type=jnp.fl...  36 us
  transfers between devices with their start and end apart: 4, of which 4 were waited for; matrix products, arithmetic and copies ran while one was open for 6% of the time, Pallas kernels for 0%

commit v1 on v0

v1 whole, which is shorter than its diff:
```python
import functools

import jax
import jax.numpy as jnp
from jax import lax
from jax.experimental import pallas as pl
from jax.experimental.pallas import tpu as pltpu
from jax.sharding import PartitionSpec as P

LN_EPS = 1e-5
CORES = 2
SIDE = 4
OFFSETS = (0, -1, 1, 2)
VMEM_LIMIT = 60 * 1024 * 1024
MESH = pl.DeviceIdType.MESH


def normalize(hidden):
    h_f32 = hidden.astype(jnp.float32)
    centred = h_f32 - jnp.mean(h_f32, axis=-1, keepdims=True)
    inv_std = lax.rsqrt(jnp.mean(centred * centred, axis=-1, keepdims=True) + LN_EPS)
    return centred * inv_std, inv_std


def place():
    rank = lax.axis_index('tp')
    return rank // (SIDE * CORES), (rank // CORES) % SIDE, rank % CORES


def device(y, x, c):
    return {'tp': (((y + SIDE) % SIDE) * SIDE + (x + SIDE) % SIDE) * CORES + c}


def gather_kernel(h_ref, e_ref, gain_ref, bias_ref, code_ref, x_all, e_all, c_all, x_buf, send, recv, local):
    y, x, c = place()
    xp, xm, xo = device(y, x + 1, c), device(y, x - 1, c), device(y, x + 2, c)
    yp, ym, yo = device(y + 1, x, c), device(y - 1, x, c), device(y + 2, x, c)
    pc = device(y, x, 1 - c)
    barrier = pltpu.get_barrier_semaphore()
    peers = (xp, xm, xo, yp, ym, yo, pc)
    for peer in peers:
        pl.semaphore_signal(barrier, inc=1, device_id=peer, device_id_type=MESH)
    pl.semaphore_wait(barrier, len(peers))

    rows = h_ref.shape[0]
    lo, hi = pl.ds(0, rows // 2), pl.ds(rows // 2, rows // 2)

    def remote(i, src, dst, to):
        return pltpu.make_async_remote_copy(src_ref=src, dst_ref=dst, send_sem=send.at[i], recv_sem=recv.at[i], device_id=to, device_id_type=MESH)

    def ring(first, src, all_ref, unit, up, down):
        return [
            remote(first + 0, src.at[lo], all_ref.at[unit, lo], up),
            remote(first + 1, src.at[hi], all_ref.at[2 * unit, hi], down),
            remote(first + 2, src.at[hi], all_ref.at[unit, hi], up),
            remote(first + 3, src.at[lo], all_ref.at[2 * unit, lo], down),
            remote(first + 4, all_ref.at[unit, lo], all_ref.at[3 * unit, lo], up),
            remote(first + 5, all_ref.at[2 * unit, hi], all_ref.at[3 * unit, hi], down),
        ]

    xs = ring(0, x_all.at[0], x_all, 1, xp, xm)
    es = ring(6, e_ref, e_all, 2, yp, ym)
    swap = [
        remote(12, e_ref, e_all.at[1], pc),
        remote(13, e_all.at[2], e_all.at[3], pc),
        remote(14, e_all.at[4], e_all.at[5], pc),
        remote(15, e_all.at[6, lo], e_all.at[7, lo], pc),
        remote(16, e_all.at[6, hi], e_all.at[7, hi], pc),
    ]
    codes = [
        remote(17, code_ref, c_all.at[0, 0, 1], xp),
        remote(18, code_ref, c_all.at[0, 0, 2], xm),
        remote(19, code_ref, c_all.at[0, 0, 3], xo),
        remote(20, c_all.at[0, 0], c_all.at[0, 1], yp),
        remote(21, c_all.at[0, 0], c_all.at[0, 2], ym),
        remote(22, c_all.at[0, 0], c_all.at[0, 3], yo),
        remote(23, c_all.at[0], c_all.at[1], pc),
    ]
    keep_e = pltpu.make_async_copy(e_ref, e_all.at[0], local.at[0])
    keep_x = pltpu.make_async_copy(x_buf, x_all.at[0], local.at[1])
    keep_c = pltpu.make_async_copy(code_ref, c_all.at[0, 0, 0], local.at[2])

    for copy in es[:4] + swap[:1] + codes[:3] + [keep_e, keep_c]:
        copy.start()
    step = rows // 4

    def norm(i, carry):
        at = pl.ds(pl.multiple_of(i * step, step), step)
        x_hat, _ = normalize(h_ref[at, :])
        x_buf[at, :] = (x_hat * gain_ref[...] + bias_ref[...]).astype(x_buf.dtype)
        return carry

    lax.fori_loop(0, 4, norm, 0)
    keep_x.start()
    keep_x.wait()
    for copy in xs[:4]:
        copy.start()
    keep_c.wait()
    for copy in codes[:3]:
        copy.wait_recv()
    for copy in codes[3:6]:
        copy.start()
    es[0].wait_recv()
    es[4].start()
    es[1].wait_recv()
    es[5].start()
    xs[0].wait_recv()
    xs[4].start()
    xs[1].wait_recv()
    xs[5].start()
    es[2].wait_recv()
    swap[1].start()
    es[3].wait_recv()
    swap[2].start()
    for copy in codes[3:6]:
        copy.wait_recv()
    codes[6].start()
    es[4].wait_recv()
    swap[3].start()
    es[5].wait_recv()
    swap[4].start()
    for copy in xs[2:] + swap + codes[6:]:
        copy.wait_recv()
    for copy in xs + es + swap + codes:
        copy.wait_send()
    keep_e.wait()


def gather_call(hidden, embed, gain, bias, code):
    rows, dim = hidden.shape
    vmem, anywhere = pl.BlockSpec(memory_space=pltpu.VMEM), pl.BlockSpec(memory_space=pl.ANY)
    return pl.pallas_call(
        gather_kernel,
        out_shape=(
            jax.ShapeDtypeStruct((SIDE, rows, dim), jnp.bfloat16),
            jax.ShapeDtypeStruct((SIDE * CORES,) + embed.shape, jnp.bfloat16),
            jax.ShapeDtypeStruct((CORES, SIDE, SIDE) + code.shape, jnp.int32),
        ),
        in_specs=[vmem] * 5,
        out_specs=(anywhere,) * 3,
        scratch_shapes=[
            pltpu.VMEM((rows, dim), jnp.bfloat16),
            pltpu.SemaphoreType.DMA((24,)),
            pltpu.SemaphoreType.DMA((24,)),
            pltpu.SemaphoreType.DMA((3,)),
        ],
        compiler_params=pltpu.CompilerParams(collective_id=0, has_side_effects=True),
        cost_estimate=pl.CostEstimate(flops=10**10, bytes_accessed=10**7, transcendentals=0),
    )(hidden, embed, gain.reshape(1, dim), bias.reshape(1, dim), code)


def column_ids(col, vocab, y, x, c):
    block, within = col // vocab, col % vocab
    ring_at = block // CORES
    off = jnp.where(ring_at == 0, 0, jnp.where(ring_at == 1, SIDE - 1, ring_at - 1))
    core = (c + block % CORES) % CORES
    return ((((y + off) % SIDE) * SIDE + x) * CORES + core) * vocab + within


def logits_kernel(vocab, step, x_ref, e_ref, code_ref, ids_ref, z_ref, stat_ref):
    x = x_ref[...]
    tile = x.shape[0]
    code = code_ref[...]
    run_max = run_sum = run_tgt = None
    for at in range(0, e_ref.shape[0], step):
        z = lax.dot_general(x, e_ref[at:at + step, :], (((1,), (1,)), ((), ())), preferred_element_type=jnp.float32)
        z_ref[:, at:at + step] = z
        parts = [z[:, g:g + 128] for g in range(0, step, 128)]
        new_max = functools.reduce(jnp.maximum, parts if run_max is None else parts + [run_max])
        new_sum = functools.reduce(jnp.add, [jnp.exp(p - new_max) for p in parts])
        new_tgt = functools.reduce(jnp.add, [jnp.where(ids_ref[:, at + g:at + g + 128] == code, p, 0.0) for g, p in zip(range(0, step, 128), parts)])
        if run_max is not None:
            new_sum = new_sum + run_sum * jnp.exp(run_max - new_max)
            new_tgt = new_tgt + run_tgt
        run_max, run_sum, run_tgt = new_max, new_sum, new_tgt
    peak = jnp.max(run_max, axis=1, keepdims=True)
    norm = jnp.sum(run_sum * jnp.exp(run_max - peak), axis=1, keepdims=True)
    tgt = jnp.sum(run_tgt, axis=1, keepdims=True)
    lane = lax.broadcasted_iota(jnp.int32, (tile, 128), 1)
    stat = jnp.where(lane == 0, peak, jnp.where(lane == 1, norm, tgt))
    stat_ref[...] = stat.T[:8, :]


def logits_call(x, e, code, ids, vocab):
    (rows, dim), width = x.shape, e.shape[0]
    tile = rows // SIDE
    return pl.pallas_call(
        functools.partial(logits_kernel, vocab, 512),
        grid=(rows // tile,),
        out_shape=(jax.ShapeDtypeStruct((rows, width), jnp.float32), jax.ShapeDtypeStruct((8, rows), jnp.float32)),
        in_specs=[
            pl.BlockSpec((tile, dim), lambda i: (i, 0)),
            pl.BlockSpec((width, dim), lambda i: (0, 0), pipeline_mode=pl.Buffered(1)),
            pl.BlockSpec((tile, 1), lambda i: (i, 0)),
            pl.BlockSpec((1, width), lambda i: (0, 0)),
        ],
        out_specs=(pl.BlockSpec((tile, width), lambda i: (i, 0)), pl.BlockSpec((8, tile), lambda i: (0, i))),
        compiler_params=pltpu.CompilerParams(vmem_limit_bytes=VMEM_LIMIT),
        cost_estimate=pl.CostEstimate(flops=2 * rows * width * dim, bytes_accessed=rows * width * 4, transcendentals=rows * width),
    )(x, e, code, ids)


def lse_kernel(stat_ref, c_ref, code_ref, rows_ref, cols_ref, got, send, recv):
    y, x, c = place()
    shifts = (1, -1, 2)
    peers = [device(y, x + s, c) for s in shifts]
    barrier = pltpu.get_barrier_semaphore()
    for peer in peers:
        pl.semaphore_signal(barrier, inc=1, device_id=peer, device_id_type=MESH)
    pl.semaphore_wait(barrier, len(peers))
    copies = [
        pltpu.make_async_remote_copy(src_ref=stat_ref, dst_ref=got.at[i], send_sem=send.at[i], recv_sem=recv.at[i], device_id=peer, device_id_type=MESH)
        for i, peer in enumerate(peers)
    ]
    for copy in copies:
        copy.start()
    count = jnp.sum(jnp.sum((c_ref[...] >= 0).astype(jnp.float32), axis=0, keepdims=True), axis=1, keepdims=True)
    for copy in copies:
        copy.wait_recv()
    tokens = stat_ref.shape[1] // SIDE
    line = lax.broadcasted_iota(jnp.int32, (128, tokens), 0)
    where_of = {o % SIDE: k for k, o in enumerate(OFFSETS)}
    for k, off in enumerate(OFFSETS):
        views = [stat_ref[:, k * tokens:(k + 1) * tokens]]
        for i, s in enumerate(shifts):
            at = where_of[(off + s) % SIDE]
            views.append(got[i, :, at * tokens:(at + 1) * tokens])
        peak = functools.reduce(jnp.maximum, [v[0:1] for v in views])
        norm = functools.reduce(jnp.add, [v[1:2] * jnp.exp(v[0:1] - peak) for v in views])
        tgt = functools.reduce(jnp.add, [v[2:3] for v in views])
        code = code_ref[:, k * tokens:(k + 1) * tokens]
        weight = jnp.where(code >= 0, 1.0, 0.0)
        lse = peak + jnp.log(norm)
        cols = jnp.where(line == 0, lse, jnp.where(line == 1, weight / count, jnp.where(line == 2, code, 0.0)))
        cols_ref[k * tokens:(k + 1) * tokens, :] = cols.T
        line8 = line[:8]
        rows_ref[:, k * tokens:(k + 1) * tokens] = jnp.where(line8 == 0, (lse - tgt) * weight, jnp.where(line8 == 1, count, 0.0))
    for copy in copies:
        copy.wait_send()


def lse_call(stat, c_all, code_row):
    vmem = pl.BlockSpec(memory_space=pltpu.VMEM)
    return pl.pallas_call(
        lse_kernel,
        out_shape=(jax.ShapeDtypeStruct(stat.shape, jnp.float32), jax.ShapeDtypeStruct((stat.shape[1], 128), jnp.float32)),
        in_specs=[vmem] * 3,
        out_specs=(vmem, vmem),
        scratch_shapes=[pltpu.VMEM((3,) + stat.shape, jnp.float32), pltpu.SemaphoreType.DMA((3,)), pltpu.SemaphoreType.DMA((3,))],
        compiler_params=pltpu.CompilerParams(collective_id=1, has_side_effects=True),
        cost_estimate=pl.CostEstimate(flops=10**9, bytes_accessed=10**5, transcendentals=0),
    )(stat, c_all, code_row)


PHASES = (((3, 0), (3, 1)), ((2, 1), (1, 0)), ((2, 0), (1, 1)), ((0, 0), (0, 1)))


def backward_kernel(z_any, x_any, e_any, cols_ref, rows_ref, ids_ref, h_ref, gain_ref, dh_ref, sums_ref, de_any, xr, yr, dr, dz, xa, ea, xs, ys, ss, more, red, load, zsem, xsend, xrecv, ysend, yrecv, ssend, srecv, keep, rsend, rrecv):
    y, x, c = place()
    up = (device(y, x + 1, c), device(y + 1, x, c))
    down = (device(y, x - 1, c), device(y - 1, x, c))
    other = device(y, x, 1 - c)
    barrier = pltpu.get_barrier_semaphore()
    far = (device(y, x + 2, c), device(y + 2, x, c))
    for peer in up + down + far + (other,):
        pl.semaphore_signal(barrier, inc=1, device_id=peer, device_id_type=MESH)

    tokens, dim = h_ref.shape
    half = tokens // 2
    vocab = ea.shape[0] // (SIDE * CORES)
    wide = 512

    slots, span = ys.shape[0], 1024
    n_span = z_any.shape[1] // span
    per_block = 2 * n_span
    n_z = SIDE * per_block

    def spot(q):
        block, part = SIDE - 1 - q // per_block, (q // n_span) % 2
        return pl.multiple_of(block * tokens + part * half, half), pl.multiple_of((q % n_span) * span, span)

    def fetch(q):
        row, col = spot(q)
        return pltpu.make_async_copy(z_any.at[pl.ds(row, half), pl.ds(col, span)], ys.at[q % slots, :, pl.ds(0, span)], zsem.at[q % slots])

    loads = [pltpu.make_async_copy(e_any, ea, load.at[2]), pltpu.make_async_copy(x_any, xa, load.at[3])]
    for q in range(slots - 1):
        fetch(q).start()
    loads[0].start()

    def d_logits(q, carry):
        @pl.when(q + slots - 1 < n_z)
        def _():
            fetch(q + slots - 1).start()

        fetch(q).wait()
        row, col = spot(q)
        at = pl.ds(row, half)
        stat = cols_ref[at, :]
        lse, scale, code = stat[:, 0:1], stat[:, 1:2], stat[:, 2:3]
        for v in range(0, span, wide):
            here = pl.ds(pl.multiple_of(col + v, wide), wide)
            hot = jnp.where(ids_ref[:, here] == code, 1.0, 0.0)
            dz[at, here] = ((jnp.exp(ys[q % slots, :, v:v + wide] - lse) - hot) * scale).astype(dz.dtype)
        return carry

    lax.fori_loop(0, per_block, d_logits, 0)
    loads[1].start()
    pl.semaphore_wait(barrier, 7)

    def remote(src, dst, send, recv, to):
        return pltpu.make_async_remote_copy(src_ref=src, dst_ref=dst, send_sem=send, recv_sem=recv, device_id=to, device_id_type=MESH)

    xc, yc, sc = [], [], []
    for p in range(3):
        s = 2 * (p % 2)
        xc.append([remote(xs.at[s + j], xr.at[2 * p + j], xsend.at[2 * p + j], xrecv.at[2 * p + j], (up, down)[j][0]) for j in range(2)])
        yc.append([remote(ys.at[s + j], yr.at[2 * p + j], ysend.at[2 * p + j], yrecv.at[2 * p + j], (up, down)[j][1]) for j in range(2)])
    for p in range(4):
        sc.append([remote(ss.at[j], dr.at[2 * p + j], ssend.at[2 * p + j], srecv.at[2 * p + j], other) for j in range(2)])

    def add(dst, terms):
        for group in zip(*terms):
            copies = [pltpu.make_async_copy(ref, more.at[j], load.at[j]) for j, ref in enumerate(group)]
            for copy in copies:
                copy.start()
            for copy in copies:
                copy.wait()
            for j in range(2):
                dst[j][...] = dst[j][...] + more[j]

    def pick(j, pair):
        return jnp.where(j == 0, pair[0], pair[1])

    def x_tiles(p, s):
        at = [block * tokens + part * half for block, part in PHASES[p]]

        def tile(i, carry):
            j, n = i // (dim // wide), i % (dim // wide)
            r = pl.ds(pl.multiple_of(pick(j, at), half), half)
            cols = pl.ds(pl.multiple_of(n * wide, wide), wide)
            xs[s + j, :, cols] = lax.dot_general(dz[r, :], ea[:, cols], (((1,), (0,)), ((), ())), preferred_element_type=jnp.float32)
            return carry

        lax.fori_loop(0, 2 * (dim // wide), tile, 0)

    def y_tiles(p, core, out, s):
        part = vocab // 2
        at = [(block * CORES + core) * vocab + h * part for block, h in PHASES[p]]

        def tile(i, carry):
            j, n = i // (dim // wide), i % (dim // wide)
            r = pl.ds(pl.multiple_of(pick(j, at), part), part)
            cols = pl.ds(pl.multiple_of(n * wide, wide), wide)
            out[s + j, :, cols] = lax.dot_general(dz[:, r], xa[:, cols], (((0,), (0,)), ((), ())), preferred_element_type=jnp.float32)
            return carry

        lax.fori_loop(0, 2 * (dim // wide), tile, 0)

    loads[0].wait()
    for p in range(4):
        s = 2 * (p % 2)
        if p >= 2:
            for copy in xc[p - 2]:
                copy.wait_send()
        x_tiles(p, s)
        if p == 2:
            for copy in xc[0]:
                copy.wait_recv()
            add([xs.at[s], xs.at[s + 1]], [[xr.at[0]], [xr.at[1]]])
        if p < 3:
            for copy in xc[p]:
                copy.start()
        if p == 0:
            lax.fori_loop(per_block, n_z, d_logits, 0)
            loads[1].wait()
        if p >= 1:
            for copy in sc[p - 1]:
                copy.wait_send()
        y_tiles(p, 1, ss, 0)
        for copy in sc[p]:
            copy.start()
        if p >= 2:
            for copy in yc[p - 2]:
                copy.wait_send()
        y_tiles(p, 0, ys, s)
        for copy in sc[p]:
            copy.wait_recv()
        add([ys.at[s], ys.at[s + 1]], [[dr.at[2 * p]], [dr.at[2 * p + 1]]])
        if p == 2:
            for copy in yc[0]:
                copy.wait_recv()
            add([ys.at[s], ys.at[s + 1]], [[yr.at[0]], [yr.at[1]]])
        if p < 3:
            for copy in yc[p]:
                copy.start()

    for copy in xc[1] + xc[2]:
        copy.wait_recv()
    add([xs.at[2], xs.at[3]], [[xr.at[4], xr.at[3]], [xr.at[2], xr.at[5]]])
    step = half // 4
    sums_ref[...] = jnp.zeros(sums_ref.shape, jnp.float32)

    def norm_back(i, carry):
        j, r = i // 4, i % 4
        at = pl.ds(pl.multiple_of(i * step, step), step)
        d_normed = xs[2 + j, pl.ds(pl.multiple_of(r * step, step), step), :]
        x_hat, inv_std = normalize(h_ref[at, :])
        g = d_normed * gain_ref[...]
        centre = jnp.mean(g, axis=-1, keepdims=True)
        proj = jnp.mean(g * x_hat, axis=-1, keepdims=True)
        dh_ref[at, :] = (inv_std * (g - centre - x_hat * proj)).astype(dh_ref.dtype)
        sums_ref[0:1, :] += jnp.sum(d_normed * x_hat, axis=0, keepdims=True)
        sums_ref[1:2, :] += jnp.sum(d_normed, axis=0, keepdims=True)
        return carry

    lax.fori_loop(0, 8, norm_back, 0)
    sums_ref[2:3, 0:128] = functools.reduce(jnp.add, [rows_ref[0:1, g:g + 128] for g in range(0, tokens, 128)])

    stages = ((x, [device(y, x + d, c) for d in (1, -1, 2)]), (y, [device(y + d, x, c) for d in (1, -1, 2)]), (c, [other]))
    k = 0
    for stage, (pos, peers) in enumerate(stages):
        red[stage, pos] = sums_ref[...]
        copies = []
        for peer in peers:
            copies.append(remote(red.at[stage, pos], red.at[stage, pos], rsend.at[k], rrecv.at[k], peer))
            k += 1
        for copy in copies:
            copy.start()
        for copy in copies:
            copy.wait_recv()
        sums_ref[...] = functools.reduce(jnp.add, [red[stage, i] for i in range(len(peers) + 1)])
        for copy in copies:
            copy.wait_send()

    for copy in yc[1] + yc[2]:
        copy.wait_recv()
    add([ys.at[2], ys.at[3]], [[yr.at[4], yr.at[3]], [yr.at[2], yr.at[5]]])
    outs = [pltpu.make_async_copy(ys.at[2 + j], de_any.at[pl.ds(j * (vocab // 2), vocab // 2)], keep.at[j]) for j in range(2)]
    for copy in outs:
        copy.start()
    for copy in outs:
        copy.wait()
    for copy in xc[2] + yc[2] + sc[3]:
        copy.wait_send()


def backward_call(z, x, e, cols, rows, ids, hidden, gain):
    tokens, dim = hidden.shape
    vocab = e.shape[0] // (SIDE * CORES)
    vmem, anywhere = pl.BlockSpec(memory_space=pltpu.VMEM), pl.BlockSpec(memory_space=pl.ANY)
    f32, tile = jnp.float32, (tokens // 2, dim)
    sem = pltpu.SemaphoreType.DMA
    out = pl.pallas_call(
        backward_kernel,
        out_shape=(
            jax.ShapeDtypeStruct(hidden.shape, jnp.bfloat16),
            jax.ShapeDtypeStruct((8, dim), f32),
            jax.ShapeDtypeStruct((vocab, dim), f32),
            jax.ShapeDtypeStruct((6,) + tile, f32),
            jax.ShapeDtypeStruct((6,) + tile, f32),
            jax.ShapeDtypeStruct((8,) + tile, f32),
        ),
        in_specs=[anywhere] * 3 + [vmem] * 5,
        out_specs=(vmem, vmem) + (anywhere,) * 4,
        scratch_shapes=[
            pltpu.VMEM(z.shape, jnp.bfloat16),
            pltpu.VMEM(x.shape, x.dtype),
            pltpu.VMEM(e.shape, e.dtype),
            pltpu.VMEM((4,) + tile, f32),
            pltpu.VMEM((4,) + tile, f32),
            pltpu.VMEM((2,) + tile, f32),
            pltpu.VMEM((2,) + tile, f32),
            pltpu.VMEM((3, SIDE, 8, dim), f32),
            sem((4,)), sem((4,)), sem((6,)), sem((6,)), sem((6,)), sem((6,)), sem((8,)), sem((8,)), sem((2,)), sem((7,)), sem((7,)),
        ],
        compiler_params=pltpu.CompilerParams(collective_id=2, has_side_effects=True, vmem_limit_bytes=67043328),
        cost_estimate=pl.CostEstimate(flops=4 * z.size * dim, bytes_accessed=10**8, transcendentals=0),
    )(z, x, e, cols, rows, ids, hidden, gain.reshape(1, dim))
    return out[:3]


def solution(mesh):
    group = mesh.shape['tp']
    assert group == SIDE * SIDE * CORES

    def body(hidden, ln_gain, ln_bias, embed, targets, loss_mask):
        tokens, dim = hidden.shape
        vocab = embed.shape[0]
        rank = lax.axis_index('tp')
        y, x, c = rank // (SIDE * CORES), (rank // CORES) % SIDE, rank % CORES
        f32 = jnp.float32

        code = jnp.where(loss_mask > 0, targets, -1)
        code = jnp.pad(code.reshape(-1, 128), ((0, 8 - tokens // 128), (0, 0)), constant_values=-1)
        x_all, e_all, c_all = gather_call(hidden, embed, ln_gain, ln_bias, code)
        n_all, v_all = SIDE * tokens, SIDE * CORES * vocab
        x_all, e_all = x_all.reshape(n_all, dim), e_all.reshape(v_all, dim)
        codes = c_all[0, 0, :, :tokens // 128].reshape(n_all)
        code_col = codes[:, None]
        ids = column_ids(lax.broadcasted_iota(jnp.int32, (1, v_all), 1), vocab, y, x, c)
        logits, stat = logits_call(x_all, e_all, code_col, ids, vocab)
        rows, cols = lse_call(stat, c_all.reshape(-1, 128), codes.astype(f32).reshape(1, n_all))
        own_loss = rows[0, :tokens]
        d_hidden, sums, d_embed = backward_call(logits, x_all, e_all, cols, rows, ids.astype(f32), hidden, ln_gain)
        mean_loss = (jnp.sum(sums[2, :128]) / rows[1, 0]).reshape(1)
        return own_loss, mean_loss, d_hidden, d_embed, sums[0], sums[1]

    token_rows = P(('dp', 'tp'))
    token_mat = P(('dp', 'tp'), None)
    return jax.shard_map(body, mesh=mesh, in_specs=(token_mat, P(), P(), P('tp', None), token_rows, token_rows), out_specs=(token_rows, P('dp'), token_mat, token_mat, P('dp'), P('dp')), check_vma=False)
```

time: 895 us -> 289 us (0.32)
  waiting for transfers between devices: 569 us -> 0 us
  Pallas kernels: 0 us -> 266 us
  blocking collectives: 152 us -> 0 us
  matrix products: 121 us -> 0 us
  other arithmetic: 33.5 us -> 4.07 us
  between operations: 16.5 us -> 3.17 us
  local copies, waits for them, and re-layouts: 2.45 us -> 14.9 us
    reduce_scatter x1 -> x0, waiting for transfers between devices: 351 us -> none  [body(): d_normed = lax.psum_scatter(d_part, 'tp', scatter_dimension=0, tiled=True)]
    pallas_call x0 -> x4, Pallas kernels: none -> 266 us  [the longest x1 154 us: backward_call(): pl.pallas_call(backward_kernel, out_shape=(jax.ShapeDtypeStruct(hidden.sh...]
    all_gather x1 -> x0, waiting for transfers between devices: 124 us -> none  [body(): gathered = lax.all_gather(normed, 'tp', tiled=True)]
    dot_general x3 -> x0, matrix products: 121 us -> none  [the longest x1 48.6 us: body(): jnp.einsum('sv,vd->sd', d_logits, embed, preferred_element_type=jnp.float32)]
    psum x2 -> x0, blocking collectives: 92.2 us -> none  [the longest x1 46.8 us: body(): count = lax.psum(jnp.sum(loss_mask.astype(jnp.float32)), 'tp')]
    pmax x1 -> x0, waiting for transfers between devices: 73.6 us -> none  [body(): global_max = lax.pmax(local_max, 'tp')]
    all_gather x2 -> x0, blocking collectives: 59.7 us -> none  [the longest x1 32.9 us: body(): all_targets = lax.all_gather(targets, 'tp', tiled=True)]
    reduce_sum x6 -> x1, other arithmetic: 25.9 us -> 1.29 us  [body(): mean_loss = (jnp.sum(sums[2, :128]) / rows[1, 0]).reshape(1)]
  transfers between devices with their start and end apart: 4 -> 0, of which waited for: 4 -> 0; matrix products, arithmetic and copies ran while one was open for 6% -> 0% of each run, Pallas kernels for 0% -> 0%
where the time goes in v1:
time: 289 us; the launch traced here: 288 us
  Pallas kernels  266 us (92%)
  local copies, waits for them, and re-layouts  14.9 us (5%)
  other arithmetic  4.07 us (1%)
  between operations  3.17 us (1%)
    pallas_call x1, Pallas kernels, backward_call(): pl.pallas_call(backward_kernel, out_shape=(jax.ShapeDtypeStruct(hidden.sh...  154 us
    pallas_call x1, Pallas kernels, gather_call(): pl.pallas_call(gather_kernel, out_shape=(jax.ShapeDtypeStruct((SIDE, rows...  66.3 us
    pallas_call x1, Pallas kernels, logits_call(): pl.pallas_call(functools.partial(logits_kernel, vocab, 512), grid=(rows /...  37.1 us
    pallas_call x1, Pallas kernels, lse_call(): pl.pallas_call(lse_kernel, out_shape=(jax.ShapeDtypeStruct(stat.shape, jn...  8.74 us
    unnamed x2, local copies, waits for them, and re-layouts  6.41 us

profile of v1, /device:TPU:97, one launch (start us, length us, event | category | flops | bytes accessed | tf_op | source)
XLA Modules:
  0.0 288.2 jit_solution(1575565177337133019)
XLA Ops:
  0.7 0.8 fusion
  1.4 1.3 reshape.348.gain_ref
  2.7 0.7 select_bitcast_fusion
  3.4 0.6 pad.4.code_ref
  4.0 1.3 reshape.349.bias_ref
  5.3 66.3 %shard_map.109 = (bf16[4,512,1536]{2,1,0:T(8,128)(2,1)}, bf16[8,512,1536]{2,1,0:T(8,128)(2,1)}, s32[2,4,4,8,128]{4,3,2,1,0:T(8,128)}) custom-call(bf16[512,1536]{1,0:T(8,128)(2,1)} %h_ref.3, bf16[512,1536]{1,0:T(8,128)(2,1)} %e_ref.1, f32[1,1536]{1,0:T(1,128)} %reshape.348.gain_ref, f32[1,1536]{1,0:T(1,128)} %reshape.349.bias_ref, s32[8,128]{1,0:T(8,128)} %pad.4.code_ref), custom_call_target="tpu_custom_call" | custom-call | flops 10000000000 | bytes 10000000 | tf_op jit(solution)/shard_map/pallas_call | solution.py:132
  71.7 1.3 slice_convert_fusion
  73.0 1.3 copy.12.code_ref
  74.3 37.1 %shard_map.110 = (f32[2048,4096]{1,0:T(8,128)}, f32[8,2048]{1,0:T(8,128)}) custom-call(bf16[2048,1536]{1,0:T(8,128)(2,1)} %bitcast.16, bf16[4096,1536]{1,0:T(8,128)(2,1)} %bitcast.14, s32[2048,1]{1,0:T(8,128)} %copy.12.code_ref, s32[1,4096]{1,0:T(1,128)} %get-tuple-element.30.ids_ref), custom_call_target="tpu_custom_call" | custom-call | flops 25769803776 | bytes 33554432 | tf_op jit(solution)/shard_map/pallas_call | solution.py:187
  111.5 8.7 %shard_map.111 = (f32[8,2048]{1,0:T(8,128)}, f32[2048,128]{1,0:T(8,128)}) custom-call(f32[8,2048]{1,0:T(8,128)} %get-tuple-element.19.stat_ref, s32[256,128]{1,0:T(8,128)} %bitcast.13, f32[1,2048]{1,0:T(1,128)} %bitcast.11), custom_call_target="tpu_custom_call" | custom-call | flops 1000000000 | bytes 100000 | tf_op jit(solution)/shard_map/pallas_call | solution.py:244
  120.2 153.8 %shard_map.112 = (bf16[512,1536]{1,0:T(8,128)(2,1)}, f32[8,1536]{1,0:T(8,128)}, f32[512,1536]{1,0:T(8,128)}, f32[6,256,1536]{2,1,0:T(8,128)}, f32[6,256,1536]{2,1,0:T(8,128)}, /*index=5*/f32[8,256,1536]{2,1,0:T(8,128)}) custom-call(f32[2048,4096]{1,0:T(8,128)} %get-tuple-element.21.z_any, bf16[2048,1536]{1,0:T(8,128)(2,1)} %bitcast.17, ...), custom_call_target="tpu_custom_call" | custom-call | flops 51539607552 | bytes 100000000 | tf_op jit(solution)/shard_map/pallas_call | solution.py:454
  274.0 1.5 slice_reduce_fusion
  275.5 1.3 slice_reduce_fusion.2
  276.8 1.2 slice.21
  279.4 1.3 slice.19
  280.7 2.7 copy.15
  283.3 3.8 %copy.16 = f32[512,1536]{1,0:T(8,128)} copy(f32[512,1536]{1,0:T(8,128)} %get-tuple-element.41) | data formatting | bytes 6291456

commit v2 on v0

v2 whole, which is shorter than its diff:
```python
import functools

import jax
import jax.numpy as jnp
from jax import lax
from jax.experimental import pallas as pl
from jax.experimental.pallas import tpu as pltpu
from jax.sharding import PartitionSpec as P

LN_EPS = 1e-5
CORES = 2
SIDE = 4
OFFSETS = (0, -1, 1, 2)
VMEM_LIMIT = 67043328
MESH = pl.DeviceIdType.MESH
BOTH = (0, 1)
LANES = 128


def row_sum(v):
    return jnp.sum(v, axis=1, keepdims=True)


def row_mean(v):
    return jnp.mean(v, axis=-1, keepdims=True)


def col_sum(v):
    return jnp.sum(v, axis=0, keepdims=True)


def dot(a, b, of_a, of_b):
    return lax.dot_general(a, b, (((of_a,), (of_b,)), ((), ())), preferred_element_type=jnp.float32)


def normalize(hidden):
    h_f32 = hidden.astype(jnp.float32)
    centred = h_f32 - row_mean(h_f32)
    inv_std = lax.rsqrt(row_mean(centred * centred) + LN_EPS)
    return centred * inv_std, inv_std


def place():
    rank = lax.axis_index('tp')
    return rank // (SIDE * CORES), (rank // CORES) % SIDE, rank % CORES


def device(y, x, c):
    return {'tp': (((y + SIDE) % SIDE) * SIDE + (x + SIDE) % SIDE) * CORES + c}


def column_ids(col, vocab, y, x, c):
    block, within = col // vocab, col % vocab
    ring_at = block // CORES
    off = jnp.where(ring_at == 0, 0, jnp.where(ring_at == 1, SIDE - 1, ring_at - 1))
    core = (c + block % CORES) % CORES
    return ((((y + off) % SIDE) * SIDE + x) * CORES + core) * vocab + within


PHASES = (((3, 0), (3, 1)), ((2, 1), (1, 0)), ((2, 0), (1, 1)), ((0, 0), (0, 1)))


def step_kernel(
    h_ref, e_any, affine_ref, code_any, ids_ref,
    dh_ref, sums_ref, rows_ref, de_any, z_any, xr, yr, dr,
    dz, xa, ea, xs, ys, ss, more, red, cols_ref, c_all, got, stat_ref,
    load, zsem, gsend, grecv, lsend, lrecv, xsend, xrecv, ysend, yrecv, ssend, srecv, keep, rsend, rrecv, osend, orecv,
):
    y, x, c = place()
    up = (device(y, x + 1, c), device(y + 1, x, c))
    down = (device(y, x - 1, c), device(y - 1, x, c))
    opposite = (device(y, x + 2, c), device(y + 2, x, c))
    other = device(y, x, 1 - c)
    barrier = pltpu.get_barrier_semaphore()
    for peer in up + down + opposite + (other,):
        pl.semaphore_signal(barrier, inc=1, device_id=peer, device_id_type=MESH)

    tokens, dim = h_ref.shape
    half = tokens // 2
    vocab = ea.shape[0] // (SIDE * CORES)
    wide = 512
    f32 = jnp.float32
    slots, span = ys.shape[0], CORES * vocab

    def remote(src, dst, send, recv, to):
        return pltpu.make_async_remote_copy(src_ref=src, dst_ref=dst, send_sem=send, recv_sem=recv, device_id=to, device_id_type=MESH)

    def xat(block, part=None):
        return xa.at[pl.ds(block * tokens, tokens)] if part is None else xa.at[pl.ds(block * tokens + part * half, half)]

    def eat(block, part=None):
        return ea.at[pl.ds(block * vocab, vocab)] if part is None else ea.at[pl.ds(block * vocab + part * (vocab // 2), vocab // 2)]

    def e_own(part):
        return e_any.at[pl.ds(part * (vocab // 2), vocab // 2)]

    tags = iter(range(gsend.shape[0]))

    def moving(src, dst, to):
        tag = next(tags)
        return remote(src, dst, gsend.at[tag], grecv.at[tag], to)

    def ring(own, at, unit, to_up, to_down):
        return [
            moving(own(0), at(unit, 0), to_up),
            moving(own(1), at(2 * unit, 1), to_down),
            moving(own(1), at(unit, 1), to_up),
            moving(own(0), at(2 * unit, 0), to_down),
            moving(at(unit, 0), at(3 * unit, 0), to_up),
            moving(at(2 * unit, 1), at(3 * unit, 1), to_down),
        ]

    gx = ring(lambda part: xat(0, part), xat, 1, up[0], down[0])
    ge = ring(e_own, eat, 2, up[1], down[1])
    swap = [
        moving(e_any, eat(1), other),
        moving(eat(2), eat(3), other),
        moving(eat(4), eat(5), other),
        moving(eat(6, 0), eat(7, 0), other),
        moving(eat(6, 1), eat(7, 1), other),
    ]
    codes = [
        moving(code_any, c_all.at[0, 0, 1], up[0]),
        moving(code_any, c_all.at[0, 0, 2], down[0]),
        moving(code_any, c_all.at[0, 0, 3], opposite[0]),
        moving(c_all.at[0, 0], c_all.at[0, 1], up[1]),
        moving(c_all.at[0, 0], c_all.at[0, 2], down[1]),
        moving(c_all.at[0, 0], c_all.at[0, 3], opposite[1]),
        moving(c_all.at[0], c_all.at[1], other),
    ]
    keep_e = pltpu.make_async_copy(e_any, eat(0), load.at[0])
    keep_c = pltpu.make_async_copy(code_any, c_all.at[0, 0, 0], load.at[1])
    keep_e.start()
    keep_c.start()
    pl.semaphore_wait(barrier, 7)
    for copy in ge[:4] + swap[:1] + codes[:3]:
        copy.start()
    step = half // 4

    def norm(i, carry):
        at = pl.ds(pl.multiple_of(i * step, step), step)
        x_hat, _ = normalize(h_ref[at, :])
        xa[at, :] = (x_hat * affine_ref[0:1, :] + affine_ref[1:2, :]).astype(xa.dtype)
        return carry

    lax.fori_loop(0, 8, norm, 0)

    halves = 2 * SIDE
    for slot in range(2):
        for hb in range(halves // 2):
            for kind, value in enumerate((-jnp.inf, 0.0, 0.0)):
                lane = (3 * hb + kind) * LANES
                ss[slot, :, lane:lane + LANES] = jnp.full((half, LANES), value, f32)
    for copy in gx[:4]:
        copy.start()
    keep_c.wait()
    for copy in codes[:3]:
        copy.wait_recv()
    for copy in codes[3:6]:
        copy.start()

    for block in range(SIDE):
        for r in range(tokens // LANES):
            hb, at = (block * tokens + r * LANES) // half, (r * LANES) % half
            more[0, at:at + LANES, hb * LANES:(hb + 1) * LANES] = jnp.broadcast_to(c_all[0, 0, block, r:r + 1, :].astype(f32), (LANES, LANES)).T

    def z_out(u, b, k, j):
        rows = pl.ds(pl.multiple_of(b * tokens + j * half, half), half)
        cols = pl.ds(pl.multiple_of(k * span, span), span)
        s = (2 * u) % slots + j
        return pltpu.make_async_copy(ys.at[s, :, pl.ds(0, span)], z_any.at[rows, cols], zsem.at[s])

    def logits(u, b, k):
        @pl.when(u >= 2)
        def _():
            for j in BOTH:
                z_out(u, b, k, j).wait()

        at = pl.ds(pl.multiple_of(b * tokens, tokens), tokens)
        s = (2 * u) % slots
        for n in range(span // wide):
            ids_at = pl.ds(pl.multiple_of(k * span + n * wide, wide), wide)
            e_at = pl.ds(pl.multiple_of(k * span + n * wide, wide), wide)
            z = dot(xa[at, :], ea[e_at, :], 1, 1)
            ids = ids_ref[:, ids_at]
            for j in BOTH:
                zj = z[j * half:(j + 1) * half]
                ys[s + j, :, n * wide:(n + 1) * wide] = zj
                hb = 2 * b + j
                slot, lane = hb // SIDE, (hb % SIDE) * 3 * LANES
                lanes = [pl.ds(pl.multiple_of(lane + kind * LANES, LANES), LANES) for kind in range(3)]
                code = more[0, :, pl.ds(pl.multiple_of(hb * LANES, LANES), LANES)]
                old_max = ss[slot, :, lanes[0]]
                parts = [zj[:, g:g + LANES] for g in range(0, wide, LANES)]
                new_max = functools.reduce(jnp.maximum, parts + [old_max])
                new_sum = ss[slot, :, lanes[1]] * jnp.exp(old_max - new_max)
                ss[slot, :, lanes[1]] = functools.reduce(jnp.add, [new_sum] + [jnp.exp(part - new_max) for part in parts])
                hits = [jnp.where(ids[:, g:g + LANES] == code, part, 0.0) for g, part in zip(range(0, wide, LANES), parts)]
                ss[slot, :, lanes[2]] = functools.reduce(jnp.add, [ss[slot, :, lanes[2]]] + hits)
                ss[slot, :, lanes[0]] = new_max
        for j in BOTH:
            z_out(u, b, k, j).start()

    keep_e.wait()
    swap[0].wait_recv()
    logits(0, 0, 0)
    ge[0].wait_recv()
    ge[4].start()
    ge[1].wait_recv()
    ge[5].start()
    gx[0].wait_recv()
    gx[4].start()
    gx[1].wait_recv()
    gx[5].start()
    ge[2].wait_recv()
    swap[1].start()
    ge[3].wait_recv()
    swap[2].start()
    for copy in codes[3:6]:
        copy.wait_recv()
    codes[6].start()
    for copy in gx[2:4] + swap[1:3]:
        copy.wait_recv()

    def near(u, carry):
        logits(u, u // 3, u % 3)
        return carry

    lax.fori_loop(1, 8, near, 0)
    ge[4].wait_recv()
    swap[3].start()
    ge[5].wait_recv()
    swap[4].start()
    lax.fori_loop(8, 9, near, 0)
    gx[4].wait_recv()
    gx[5].wait_recv()

    def far_tokens(u, carry):
        logits(u, SIDE - 1, u - 9)
        return carry

    lax.fori_loop(9, 12, far_tokens, 0)
    swap[3].wait_recv()
    swap[4].wait_recv()

    def far_vocab(u, carry):
        logits(u, u - 12, SIDE - 1)
        return carry

    lax.fori_loop(12, 16, far_vocab, 0)
    codes[6].wait_recv()

    for hb in range(halves):
        lanes = [slice((3 * (hb % SIDE) + kind) * LANES, (3 * (hb % SIDE) + kind + 1) * LANES) for kind in range(3)]
        run_max, run_sum, run_tgt = (ss[hb // SIDE, :, lane] for lane in lanes)
        peak = jnp.max(run_max, axis=1, keepdims=True)
        norm_sum = row_sum(run_sum * jnp.exp(run_max - peak))
        tgt = row_sum(run_tgt)
        lane = lax.broadcasted_iota(jnp.int32, (half, LANES), 1)
        stat_ref[:, hb * half:(hb + 1) * half] = jnp.where(lane == 0, peak, jnp.where(lane == 1, norm_sum, tgt)).T[:8, :]
    shifts = (1, -1, 2)
    stats = [remote(stat_ref, got.at[i], lsend.at[i], lrecv.at[i], peer) for i, peer in enumerate((up[0], down[0], opposite[0]))]
    for copy in stats:
        copy.start()
    count = row_sum(col_sum((c_all[...].reshape(-1, LANES) >= 0).astype(f32)))
    for j in BOTH:
        z_out(14, 0, 0, j).wait()
        z_out(15, 0, 0, j).wait()
    for copy in gx + ge + swap + codes:
        copy.wait_send()
    for copy in stats:
        copy.wait_recv()
    line = lax.broadcasted_iota(jnp.int32, (LANES, half), 0)
    where_of = {o % SIDE: k for k, o in enumerate(OFFSETS)}
    for hb in range(halves):
        block, part = hb // 2, hb % 2
        views = [stat_ref[:, hb * half:(hb + 1) * half]]
        for i, shift in enumerate(shifts):
            at = (2 * where_of[(OFFSETS[block] + shift) % SIDE] + part) * half
            views.append(got[i, :, at:at + half])
        peak = functools.reduce(jnp.maximum, [v[0:1] for v in views])
        norm_sum = functools.reduce(jnp.add, [v[1:2] * jnp.exp(v[0:1] - peak) for v in views])
        tgt = functools.reduce(jnp.add, [v[2:3] for v in views])
        lse = peak + jnp.log(norm_sum)
        cols_ref[hb * half:(hb + 1) * half, :] = jnp.where(line == 0, lse, 0.0).T
        code = more[0, :, hb * LANES:(hb + 1) * LANES]
        lane = lax.broadcasted_iota(jnp.int32, (half, LANES), 1)
        weight = jnp.where(code >= 0, 1.0, 0.0)
        rest = jnp.where(lane == 1, weight / count, jnp.where(lane == 2, code, 0.0))
        cols_ref[hb * half:(hb + 1) * half, :] += rest
        if block == 0:
            weight_row = jnp.where(lane == 0, weight, 0.0).T[0:1, :]
            line8 = line[:8]
            rows_ref[:, part * half:(part + 1) * half] = jnp.where(line8 == 0, (lse - tgt) * weight_row, jnp.where(line8 == 1, count, 0.0))
    for copy in stats:
        copy.wait_send()

    n_span = z_any.shape[1] // span
    per_block = 2 * n_span
    n_z = SIDE * per_block

    def spot(q):
        block, part = SIDE - 1 - q // per_block, (q // n_span) % 2
        return pl.multiple_of(block * tokens + part * half, half), pl.multiple_of((q % n_span) * span, span)

    def fetch(q):
        row, col = spot(q)
        return pltpu.make_async_copy(z_any.at[pl.ds(row, half), pl.ds(col, span)], ys.at[q % slots, :, pl.ds(0, span)], zsem.at[q % slots])

    for q in range(slots - 1):
        fetch(q).start()

    def d_logits(q, carry):
        @pl.when(q + slots - 1 < n_z)
        def _():
            fetch(q + slots - 1).start()

        fetch(q).wait()
        row, col = spot(q)
        at = pl.ds(row, half)
        stat = cols_ref[at, :]
        lse, scale, code = (stat[:, k:k + 1] for k in range(3))
        for v in range(0, span, wide):
            here = pl.ds(pl.multiple_of(col + v, wide), wide)
            hot = jnp.where(ids_ref[:, here] == code, 1.0, 0.0)
            dz[at, here] = ((jnp.exp(ys[q % slots, :, v:v + wide] - lse) - hot) * scale).astype(dz.dtype)
        return carry

    lax.fori_loop(0, per_block, d_logits, 0)
    chunks = dim // wide

    def part_of(n):
        return pl.ds(pl.multiple_of(n * wide, wide), wide)

    def opening(kind, j, n):
        src, dst, to = ((xs, xr, (up, down)[j][0]), (ys, yr, (up, down)[j][1]), (ss, dr, other))[kind]
        tag = (kind * len(BOTH) + j) * chunks + n
        return remote(src.at[j, :, part_of(n)], dst.at[j, :, part_of(n)], osend.at[tag], orecv.at[tag], to)

    xc, yc, sc = ([[opening(kind, j, n) for n in range(chunks) for j in BOTH]] for kind in range(3))
    for p in range(1, SIDE):
        s = 2 * (p % 2)
        if p < SIDE - 1:
            xc.append([remote(xs.at[s + j], xr.at[2 * p + j], xsend.at[2 * p + j], xrecv.at[2 * p + j], (up, down)[j][0]) for j in BOTH])
            yc.append([remote(ys.at[s + j], yr.at[2 * p + j], ysend.at[2 * p + j], yrecv.at[2 * p + j], (up, down)[j][1]) for j in BOTH])
        sc.append([remote(ss.at[j], dr.at[2 * p + j], ssend.at[2 * p + j], srecv.at[2 * p + j], other) for j in BOTH])

    def two(ref, first):
        return [ref.at[first], ref.at[first + 1]]

    def add(dst, terms):
        copies = [pltpu.make_async_copy(ref, more.at[j], load.at[j]) for j, ref in enumerate(terms)]
        for copy in copies:
            copy.start()
        for copy in copies:
            copy.wait()
        for j in BOTH:
            dst[j][...] = dst[j][...] + more[j]

    def pick(j, pair):
        return jnp.where(j == 0, pair[0], pair[1])

    def x_tiles(p, s, first, last):
        at = [block * tokens + part * half for block, part in PHASES[p]]

        def tile(i, carry):
            j, n = i % 2, i // 2
            r = pl.ds(pl.multiple_of(pick(j, at), half), half)
            xs[s + j, :, part_of(n)] = dot(dz[r, :], ea[:, part_of(n)], 1, 0)
            return carry

        lax.fori_loop(2 * first, 2 * last, tile, 0)

    def y_tiles(p, core, out, s, first, last):
        part = vocab // 2
        at = [(block * CORES + core) * vocab + h * part for block, h in PHASES[p]]

        def tile(i, carry):
            j, n = i % 2, i // 2
            r = pl.ds(pl.multiple_of(pick(j, at), part), part)
            out[s + j, :, part_of(n)] = dot(dz[:, r], xa[:, part_of(n)], 0, 0)
            return carry

        lax.fori_loop(2 * first, 2 * last, tile, 0)

    def open_links(n, carry):
        x_tiles(0, 0, n, n + 1)
        for j in BOTH:
            opening(0, j, n).start()

        @pl.when(n == 0)
        def _():
            lax.fori_loop(per_block, n_z, d_logits, 0)

        y_tiles(0, 1, ss, 0, n, n + 1)
        for j in BOTH:
            opening(2, j, n).start()
        y_tiles(0, 0, ys, 0, n, n + 1)
        for j in BOTH:
            opening(2, j, n).wait_recv()
        copies = [pltpu.make_async_copy(dr.at[j, :, part_of(n)], more.at[j, :, part_of(n)], load.at[j]) for j in BOTH]
        for copy in copies:
            copy.start()
        for copy in copies:
            copy.wait()
        for j in BOTH:
            ys[j, :, part_of(n)] = ys[j, :, part_of(n)] + more[j, :, part_of(n)]
            opening(1, j, n).start()
        return carry

    lax.fori_loop(0, chunks, open_links, 0)
    for p in range(1, SIDE):
        s = 2 * (p % 2)
        if p >= 2:
            for copy in xc[p - 2]:
                copy.wait_send()
        x_tiles(p, s, 0, chunks)
        if p == 2:
            for copy in xc[0]:
                copy.wait_recv()
            add(two(xs, s), two(xr, 0))
        if p < 3:
            for copy in xc[p]:
                copy.start()
        for copy in sc[p - 1]:
            copy.wait_send()
        y_tiles(p, 1, ss, 0, 0, chunks)
        for copy in sc[p]:
            copy.start()
        if p >= 2:
            for copy in yc[p - 2]:
                copy.wait_send()
        y_tiles(p, 0, ys, s, 0, chunks)
        for copy in sc[p]:
            copy.wait_recv()
        add(two(ys, s), two(dr, 2 * p))
        if p == 2:
            for copy in yc[0]:
                copy.wait_recv()
            add(two(ys, s), two(yr, 0))
        if p < 3:
            for copy in yc[p]:
                copy.start()

    own_x, own_y = two(xs, 2), two(ys, 2)
    for own, landed, copies in ((own_x, xr, xc[1]), (own_y, yr, yc[1])):
        for copy in copies:
            copy.wait_recv()
        add(own, [landed.at[3], landed.at[2]])
    for copy in xc[2]:
        copy.wait_recv()
    add(own_x, two(xr, 4))
    step = half // 4
    sums_ref[...] = jnp.zeros(sums_ref.shape, jnp.float32)

    def norm_back(i, carry):
        j, r = i // 4, i % 4
        at = pl.ds(pl.multiple_of(i * step, step), step)
        d_normed = xs[2 + j, pl.ds(pl.multiple_of(r * step, step), step), :]
        x_hat, inv_std = normalize(h_ref[at, :])
        g = d_normed * affine_ref[0:1, :]
        centre, proj = row_mean(g), row_mean(g * x_hat)
        dh_ref[at, :] = (inv_std * (g - centre - x_hat * proj)).astype(dh_ref.dtype)
        sums_ref[0:1, :] += col_sum(d_normed * x_hat)
        sums_ref[1:2, :] += col_sum(d_normed)
        return carry

    lax.fori_loop(0, 8, norm_back, 0)
    sums_ref[2:3, 0:LANES] = functools.reduce(jnp.add, [rows_ref[0:1, g:g + LANES] for g in range(0, tokens, LANES)])

    stages = ((x, [device(y, x + d, c) for d in (1, -1, 2)]), (y, [device(y + d, x, c) for d in (1, -1, 2)]), (c, [other]))
    k = 0
    for stage, (pos, peers) in enumerate(stages):
        red[stage, pos] = sums_ref[...]
        copies = []
        for peer in peers:
            copies.append(remote(red.at[stage, pos], red.at[stage, pos], rsend.at[k], rrecv.at[k], peer))
            k += 1
        for copy in copies:
            copy.start()
        for copy in copies:
            copy.wait_recv()
        sums_ref[...] = functools.reduce(jnp.add, [red[stage, i] for i in range(len(peers) + 1)])
        for copy in copies:
            copy.wait_send()

    sums_ref[3:4, :] = jnp.broadcast_to(row_sum(sums_ref[2:3, 0:LANES]) / rows_ref[1:2, 0:1], (1, dim))

    for copy in yc[2]:
        copy.wait_recv()
    add(own_y, two(yr, 4))
    outs = [pltpu.make_async_copy(ys.at[2 + j], de_any.at[pl.ds(j * (vocab // 2), vocab // 2)], keep.at[j]) for j in BOTH]
    for copy in outs:
        copy.start()
    for copy in outs:
        copy.wait()
    for copy in xc[2] + yc[2] + sc[3]:
        copy.wait_send()


def step_call(hidden, embed, affine, code, ids):
    tokens, dim = hidden.shape
    vocab = embed.shape[0]
    n_tok, n_voc = SIDE * tokens, SIDE * CORES * vocab
    vmem, anywhere = pl.BlockSpec(memory_space=pltpu.VMEM), pl.BlockSpec(memory_space=pl.ANY)
    f32, bf16, tile = jnp.float32, jnp.bfloat16, (tokens // 2, dim)
    out = pl.pallas_call(
        step_kernel,
        out_shape=(
            jax.ShapeDtypeStruct(hidden.shape, bf16),
            jax.ShapeDtypeStruct((8, dim), f32),
            jax.ShapeDtypeStruct((8, tokens), f32),
            jax.ShapeDtypeStruct((vocab, dim), f32),
            jax.ShapeDtypeStruct((n_tok, n_voc), f32),
            jax.ShapeDtypeStruct((6,) + tile, f32),
            jax.ShapeDtypeStruct((6,) + tile, f32),
            jax.ShapeDtypeStruct((8,) + tile, f32),
        ),
        in_specs=[vmem, anywhere, vmem, anywhere, vmem],
        out_specs=(vmem, vmem, vmem) + (anywhere,) * 5,
        scratch_shapes=[
            pltpu.VMEM((n_tok, n_voc), bf16),
            pltpu.VMEM((n_tok, dim), bf16),
            pltpu.VMEM((n_voc, dim), bf16),
            pltpu.VMEM((4,) + tile, f32),
            pltpu.VMEM((4,) + tile, f32),
            pltpu.VMEM((2,) + tile, f32),
            pltpu.VMEM((2,) + tile, f32),
            pltpu.VMEM((3, SIDE, 8, dim), f32),
            pltpu.VMEM((n_tok, LANES), f32),
            pltpu.VMEM((CORES, SIDE, SIDE) + code.shape, jnp.int32),
            pltpu.VMEM((3, 8, n_tok), f32),
            pltpu.VMEM((8, n_tok), f32),
        ] + [pltpu.SemaphoreType.DMA((n,)) for n in (SIDE, SIDE, 24, 24, SIDE, SIDE) + (6,) * SIDE + (8,) * 5 + (18, 18)],
        compiler_params=pltpu.CompilerParams(collective_id=0, has_side_effects=True, vmem_limit_bytes=VMEM_LIMIT),
        cost_estimate=pl.CostEstimate(flops=6 * n_tok * n_voc * dim, bytes_accessed=10**8, transcendentals=2 * n_tok * n_voc),
    )(hidden, embed, affine, code, ids)
    return out[:4]


def solution(mesh):
    group = mesh.shape['tp']
    assert group == SIDE * SIDE * CORES

    def body(hidden, ln_gain, ln_bias, embed, targets, loss_mask):
        tokens, dim = hidden.shape
        vocab = embed.shape[0]
        rank = lax.axis_index('tp')
        y, x, c = rank // (SIDE * CORES), (rank // CORES) % SIDE, rank % CORES
        f32 = jnp.float32

        code = jnp.where(loss_mask > 0, targets, -1)
        code = jnp.pad(code.reshape(-1, LANES), ((0, 8 - tokens // LANES), (0, 0)), constant_values=-1)
        ids = column_ids(lax.broadcasted_iota(jnp.int32, (1, SIDE * CORES * vocab), 1), vocab, y, x, c).astype(f32)
        d_hidden, sums, rows, d_embed = step_call(hidden, embed, jnp.stack([ln_gain, ln_bias]), code, ids)
        own_loss = rows[0]
        return own_loss, sums[3, :1], d_hidden, d_embed, sums[0], sums[1]

    token_rows = P(('dp', 'tp'))
    token_mat = P(('dp', 'tp'), None)
    return jax.shard_map(body, mesh=mesh, in_specs=(token_mat, P(), P(), P('tp', None), token_rows, token_rows), out_specs=(token_rows, P('dp'), token_mat, token_mat, P('dp'), P('dp')), check_vma=False)
```

time: 895 us -> 244 us (0.27)
  waiting for transfers between devices: 569 us -> 0 us
  Pallas kernels: 0 us -> 230 us
  blocking collectives: 152 us -> 0 us
  matrix products: 121 us -> 0 us
  other arithmetic: 33.5 us -> 2.06 us
  between operations: 16.5 us -> 0.7 us
    reduce_scatter x1 -> x0, waiting for transfers between devices: 351 us -> none  [body(): d_normed = lax.psum_scatter(d_part, 'tp', scatter_dimension=0, tiled=True)]
    pallas_call x0 -> x1, Pallas kernels: none -> 230 us  [step_call(): pl.pallas_call(step_kernel, out_shape=(jax.ShapeDtypeStruct(hidden.shape,...]
    all_gather x1 -> x0, waiting for transfers between devices: 124 us -> none  [body(): gathered = lax.all_gather(normed, 'tp', tiled=True)]
    dot_general x3 -> x0, matrix products: 121 us -> none  [the longest x1 48.6 us: body(): jnp.einsum('sv,vd->sd', d_logits, embed, preferred_element_type=jnp.float32)]
    psum x2 -> x0, blocking collectives: 92.2 us -> none  [the longest x1 46.8 us: body(): count = lax.psum(jnp.sum(loss_mask.astype(jnp.float32)), 'tp')]
    pmax x1 -> x0, waiting for transfers between devices: 73.6 us -> none  [body(): global_max = lax.pmax(local_max, 'tp')]
    all_gather x2 -> x0, blocking collectives: 59.7 us -> none  [the longest x1 32.9 us: body(): all_targets = lax.all_gather(targets, 'tp', tiled=True)]
    reduce_sum x6 -> x0, other arithmetic: 25.9 us -> none  [the longest x1 16.2 us: body(): local_sum = jnp.sum(jnp.exp(logits - local_max[:, None]), axis=-1)]
  transfers between devices with their start and end apart: 4 -> 0, of which waited for: 4 -> 0; matrix products, arithmetic and copies ran while one was open for 6% -> 0% of each run, Pallas kernels for 0% -> 0%
where the time goes in v2:
time: 244 us; the launch traced here: 243 us
  Pallas kernels  230 us (94%)
  local copies, waits for them, and re-layouts  10.5 us (4%)
    pallas_call x1, Pallas kernels, step_call(): pl.pallas_call(step_kernel, out_shape=(jax.ShapeDtypeStruct(hidden.shape,...  230 us

profile of v2, /device:TPU:97, one launch (start us, length us, event | category | flops | bytes accessed | tf_op | source)
XLA Modules:
  0.0 243.4 jit_solution(16425876638232286237)
XLA Ops:
  0.7 0.7 select_bitcast_fusion
  1.4 0.6 pad.4.code_any
  2.0 0.7 stack.9
  2.7 0.7 stack.10
  3.4 0.6 pad_maximum_fusion.affine_ref
  4.0 0.7 fusion.2.ids_ref
  4.7 230.2 %shard_map.109 = (bf16[512,1536]{1,0:T(8,128)(2,1)}, f32[8,1536]{1,0:T(8,128)}, f32[8,512]{1,0:T(8,128)}, f32[512,1536]{1,0:T(8,128)}, f32[2048,4096]{1,0:T(8,12...) custom-call(bf16[512,1536]{1,0:T(8,128)(2,1)} %h_ref.1, bf16[512,1536]{1,0:T(8,128)(2,1)} %e_any.1, ...), custom_call_target="tpu_custom_call" | custom-call | flops 77309411328 | bytes 100000000 | tf_op jit(solution)/shard_map/pallas_call | solution.py:507
  234.9 0.0 copy-start
  234.9 1.3 slice.13
  236.3 1.3 slice.12
  237.6 1.5 slice_reduce_fusion
  239.1 2.7 %copy.14 = bf16[512,1536]{1,0:T(8,128)(2,1)} copy(bf16[512,1536]{1,0:T(8,128)(2,1)} %get-tuple-element.24) | data formatting | bytes 3145728
  241.7 0.0 copy-done
  241.7 1.7 copy.15
Async XLA Ops:
  234.9 6.8 %copy-start = (f32[512,1536]{1,0:T(8,128)S(1)}, f32[512,1536]{1,0:T(8,128)}, u32[]{:S(2)}) copy-start(f32[512,1536]{1,0:T(8,128)} %get-tuple-element.25) | copy-start | bytes 9437188

commit v3 on v2

--- a/solution.py
+++ b/solution.py
@@ -178,24 +178,24 @@
 
         at = pl.ds(pl.multiple_of(b * tokens, tokens), tokens)
         s = (2 * u) % slots
-        for n in range(span // wide):
-            ids_at = pl.ds(pl.multiple_of(k * span + n * wide, wide), wide)
-            e_at = pl.ds(pl.multiple_of(k * span + n * wide, wide), wide)
+        for n in range(span // span):
+            ids_at = pl.ds(pl.multiple_of(k * span + n * span, span), span)
+            e_at = pl.ds(pl.multiple_of(k * span + n * span, span), span)
             z = dot(xa[at, :], ea[e_at, :], 1, 1)
             ids = ids_ref[:, ids_at]
             for j in BOTH:
                 zj = z[j * half:(j + 1) * half]
-                ys[s + j, :, n * wide:(n + 1) * wide] = zj
+                ys[s + j, :, n * span:(n + 1) * span] = zj
                 hb = 2 * b + j
                 slot, lane = hb // SIDE, (hb % SIDE) * 3 * LANES
                 lanes = [pl.ds(pl.multiple_of(lane + kind * LANES, LANES), LANES) for kind in range(3)]
                 code = more[0, :, pl.ds(pl.multiple_of(hb * LANES, LANES), LANES)]
                 old_max = ss[slot, :, lanes[0]]
-                parts = [zj[:, g:g + LANES] for g in range(0, wide, LANES)]
+                parts = [zj[:, g:g + LANES] for g in range(0, span, LANES)]
                 new_max = functools.reduce(jnp.maximum, parts + [old_max])
                 new_sum = ss[slot, :, lanes[1]] * jnp.exp(old_max - new_max)
                 ss[slot, :, lanes[1]] = functools.reduce(jnp.add, [new_sum] + [jnp.exp(part - new_max) for part in parts])
-                hits = [jnp.where(ids[:, g:g + LANES] == code, part, 0.0) for g, part in zip(range(0, wide, LANES), parts)]
+                hits = [jnp.where(ids[:, g:g + LANES] == code, part, 0.0) for g, part in zip(range(0, span, LANES), parts)]
                 ss[slot, :, lanes[2]] = functools.reduce(jnp.add, [ss[slot, :, lanes[2]]] + hits)
                 ss[slot, :, lanes[0]] = new_max
         for j in BOTH:
@@ -250,6 +250,18 @@
     lax.fori_loop(12, 16, far_vocab, 0)
     codes[6].wait_recv()
 
+    n_span = z_any.shape[1] // span
+    per_block = 2 * n_span
+    n_z = SIDE * per_block
+
+    def spot(q):
+        block, part = SIDE - 1 - q // per_block, (q // n_span) % 2
+        return pl.multiple_of(block * tokens + part * half, half), pl.multiple_of((q % n_span) * span, span)
+
+    def fetch(q):
+        row, col = spot(q)
+        return pltpu.make_async_copy(z_any.at[pl.ds(row, half), pl.ds(col, span)], ys.at[q % slots, :, pl.ds(0, span)], zsem.at[q % slots])
+
     for hb in range(halves):
         lanes = [slice((3 * (hb % SIDE) + kind) * LANES, (3 * (hb % SIDE) + kind + 1) * LANES) for kind in range(3)]
         run_max, run_sum, run_tgt = (ss[hb // SIDE, :, lane] for lane in lanes)
@@ -266,6 +278,8 @@
     for j in BOTH:
         z_out(14, 0, 0, j).wait()
         z_out(15, 0, 0, j).wait()
+    for q in range(slots - 1):
+        fetch(q).start()
     for copy in gx + ge + swap + codes:
         copy.wait_send()
     for copy in stats:
@@ -294,21 +308,6 @@
             rows_ref[:, part * half:(part + 1) * half] = jnp.where(line8 == 0, (lse - tgt) * weight_row, jnp.where(line8 == 1, count, 0.0))
     for copy in stats:
         copy.wait_send()
-
-    n_span = z_any.shape[1] // span
-    per_block = 2 * n_span
-    n_z = SIDE * per_block
-
-    def spot(q):
-        block, part = SIDE - 1 - q // per_block, (q // n_span) % 2
-        return pl.multiple_of(block * tokens + part * half, half), pl.multiple_of((q % n_span) * span, span)
-
-    def fetch(q):
-        row, col = spot(q)
-        return pltpu.make_async_copy(z_any.at[pl.ds(row, half), pl.ds(col, span)], ys.at[q % slots, :, pl.ds(0, span)], zsem.at[q % slots])
-
-    for q in range(slots - 1):
-        fetch(q).start()
 
     def d_logits(q, carry):
         @pl.when(q + slots - 1 < n_z)

time: 244 us -> 243 us (level)
  no operation moved by 1% of the time
where the time goes in v3:
time: 243 us
  Pallas kernels  229 us (94%)
  local copies, waits for them, and re-layouts  10.5 us (4%)
    pallas_call x1, Pallas kernels, step_call(): pl.pallas_call(step_kernel, out_shape=(jax.ShapeDtypeStruct(hidden.shape,...  229 us

profile of v3, /device:TPU:97, one launch (start us, length us, event | category | flops | bytes accessed | tf_op | source)
XLA Modules:
  0.0 242.7 jit_solution(14682024624769660928)
XLA Ops:
  0.7 0.7 select_bitcast_fusion
  1.4 0.6 pad.4.code_any
  2.0 0.7 stack.9
  2.7 0.7 stack.10
  3.4 0.6 pad_maximum_fusion.affine_ref
  4.0 0.7 fusion.2.ids_ref
  4.7 229.5 %shard_map.109 = (bf16[512,1536]{1,0:T(8,128)(2,1)}, f32[8,1536]{1,0:T(8,128)}, f32[8,512]{1,0:T(8,128)}, f32[512,1536]{1,0:T(8,128)}, f32[2048,4096]{1,0:T(8,12...) custom-call(bf16[512,1536]{1,0:T(8,128)(2,1)} %h_ref.1, bf16[512,1536]{1,0:T(8,128)(2,1)} %e_any.1, ...), custom_call_target="tpu_custom_call" | custom-call | flops 77309411328 | bytes 100000000 | tf_op jit(solution)/shard_map/pallas_call | solution.py:506
  234.2 0.0 copy-start
  234.2 1.3 slice.13
  235.6 1.3 slice.12
  236.9 1.5 slice_reduce_fusion
  238.4 2.7 %copy.14 = bf16[512,1536]{1,0:T(8,128)(2,1)} copy(bf16[512,1536]{1,0:T(8,128)(2,1)} %get-tuple-element.24) | data formatting | bytes 3145728
  241.0 0.0 copy-done
  241.0 1.7 copy.15
Async XLA Ops:
  234.2 6.8 %copy-start = (f32[512,1536]{1,0:T(8,128)S(1)}, f32[512,1536]{1,0:T(8,128)}, u32[]{:S(2)}) copy-start(f32[512,1536]{1,0:T(8,128)} %get-tuple-element.25) | copy-start | bytes 9437188
